TPU v7x, 32 devices: a whole 2x2x4 slice. The times are simulated.
32 devices in a mesh: expert: 4 (over y, core), unit: 8 (over z, x).
Axes of the slice: x: 2, y: 2, z: 4, core: 2. Of those that a mesh axis runs over, the one named last changes fastest.
Arguments:
- a_gate: bfloat16 [4, 14336, 4096], P('expert', 'unit'), may hold values from -0.09375 to 0.09375
- a_up: bfloat16 [4, 14336, 4096], P('expert', 'unit'), may hold values from -0.09375 to 0.09375
- b_gate: bfloat16 [4, 14336, 4096], P('expert', 'unit'), may hold values from -0.09375 to 0.09375
- b_up: bfloat16 [4, 14336, 4096], P('expert', 'unit'), may hold values from -0.09375 to 0.09375
- order: int32 [4, 448], P('expert'), may hold values from 0 to 447, each once within a row
- calib: bfloat16 [128, 4096], P(('expert', 'unit')), may hold values from -6 to 6
Outputs:
- merged_gate: bfloat16 [4, 14336, 4096], P('expert', 'unit')
- merged_up: bfloat16 [4, 14336, 4096], P('expert', 'unit')
- hidden: bfloat16 [4, 14336, 128], P('expert', 'unit')
Inputs may be any that keep to these rules, and one draw needn't show every extreme that they name: Each row of order is a permutation of the 448 block numbers.
All inputs are finite; a program needn't handle non-finite values.
Results may differ from a plain program's by a relative error of at most 0.006.
Values may be sent and summed in bfloat16 or wider, within the bound.
A program may use at most 256 MiB of HBM per device.

v0:
```python
import jax
import jax.numpy as jnp
from jax import lax
from jax.sharding import PartitionSpec as P

BLOCK = 32


def average(first, second):
    return ((first.astype(jnp.float32) + second.astype(jnp.float32)) * 0.5).astype(jnp.bfloat16)


def local(a_gate, a_up, b_gate, b_up, order, calib):
    blocks = order.shape[1]
    total = blocks * BLOCK
    inverse = jnp.zeros((blocks,), jnp.int32).at[order[0]].set(jnp.arange(blocks, dtype=jnp.int32))

    def relocate(columns):
        grouped = columns.reshape(blocks, BLOCK, columns.shape[1])
        return jnp.take(grouped, inverse, axis=0).reshape(total, columns.shape[1])

    gathered = (
        lax.all_to_all(b_gate[0], "unit", split_axis=1, concat_axis=0, tiled=True),
        lax.all_to_all(b_up[0], "unit", split_axis=1, concat_axis=0, tiled=True),
    )
    returned = (
        lax.all_to_all(relocate(gathered[0]), "unit", split_axis=0, concat_axis=1, tiled=True),
        lax.all_to_all(relocate(gathered[1]), "unit", split_axis=0, concat_axis=1, tiled=True),
    )
    merged_gate = average(a_gate[0], returned[0])
    merged_up = average(a_up[0], returned[1])
    dims = (((1,), (1,)), ((), ()))
    piece = lax.all_gather(calib, ("expert", "unit"), axis=0, tiled=True)
    gate_pre = lax.dot_general(merged_gate, piece, dims, preferred_element_type=jnp.float32)
    up_pre = lax.dot_general(merged_up, piece, dims, preferred_element_type=jnp.float32)
    hidden = (jax.nn.silu(gate_pre) * up_pre).astype(jnp.bfloat16)
    return (merged_gate[None], merged_up[None], hidden[None])


def solution(mesh):
    in_specs = (
        P("expert", "unit", None),
        P("expert", "unit", None),
        P("expert", "unit", None),
        P("expert", "unit", None),
        P("expert", None),
        P(("expert", "unit"), None),
    )
    out_specs = (P("expert", "unit", None), P("expert", "unit", None), P("expert", "unit", None))
    return jax.shard_map(local, mesh=mesh, in_specs=in_specs, out_specs=out_specs, check_vma=False)
```

profile of v0, /device:TPU:0, one launch (start us, length us, event | category | flops | bytes accessed | tf_op | source)
XLA Modules:
  0.0 1635.2 jit_solution(6001479759196739935)
XLA Ops:
  7.2 18.6 %copy.22 = bf16[1,1792,4096]{1,2,0:T(8,128)(2,1)} copy(bf16[1,1792,4096]{2,1,0:T(8,128)(2,1)} %param.10) | data formatting | bytes 29360128 | tf_op args[2]
  33.1 18.6 %copy.26 = bf16[1,1792,4096]{1,2,0:T(8,128)(2,1)} copy(bf16[1,1792,4096]{2,1,0:T(8,128)(2,1)} %param.11) | data formatting | bytes 29360128 | tf_op args[3]
  51.7 299.4 %all-to-all-done = bf16[1792,8,512]{0,2,1:T(8,128)(2,1)} async-done(((bf16[1792,8,512]{0,2,1:T(8,128)(2,1)}), bf16[1792,8,512]{0,2,1:T(8,128)(2,1)}, u32[]{:S(2)}, u32[]{:S(2)}) %all-to-all-start) | async-done | bytes 14680096 | tf_op jit(solution)/shard_map/all_to_all | solution.py:23
  359.8 18.7 %copy.23 = bf16[8,1792,512]{2,1,0:T(8,128)(2,1)} copy(bf16[8,1792,512]{1,2,0:T(8,128)(2,1)} %bitcast.3) | data formatting | bytes 29360128 | tf_op jit(solution)/shard_map/all_to_all | solution.py:23
  378.5 295.4 %all-to-all-done.2 = bf16[1792,8,512]{0,2,1:T(8,128)(2,1)} async-done(((bf16[1792,8,512]{0,2,1:T(8,128)(2,1)}), bf16[1792,8,512]{0,2,1:T(8,128)(2,1)}, u32[]{:S(2)}, u32[]{:S(2)}) %all-to-all-start.2) | async-done | bytes 14680096 | tf_op jit(solution)/shard_map/all_to_all | solution.py:24
  673.8 18.7 %copy.27 = bf16[8,1792,512]{2,1,0:T(8,128)(2,1)} copy(bf16[8,1792,512]{1,2,0:T(8,128)(2,1)} %bitcast.9) | data formatting | bytes 29360128 | tf_op jit(solution)/shard_map/all_to_all | solution.py:24
  692.5 18.6 %gather_fusion = bf16[448,32,512]{2,1,0:T(8,128)(2,1)} fusion(bf16[448,32,512]{2,1,0:T(8,128)(2,1)} %bitcast.50, s32[1024]{0:T(1024)S(1)} %pad_clamp_fusion), kind=kCustom, calls=%fused_computation.clone | custom fusion | bytes 29361920 | tf_op jit(solution)/shard_map/jit(_take)/gather | solution.py:20
  711.1 18.6 %gather_fusion.1 = bf16[448,32,512]{2,1,0:T(8,128)(2,1)} fusion(bf16[448,32,512]{2,1,0:T(8,128)(2,1)} %bitcast.52, s32[1024]{0:T(1024)S(1)} %pad_clamp_fusion), kind=kCustom, calls=%fused_computation.1.clone | custom fusion | bytes 29361920 | tf_op jit(solution)/shard_map/jit(_take)/gather | solution.py:20
  729.7 17.3 %broadcast_select_fusion = (bf16[448,32,512]{2,1,0:T(8,128)(2,1)S(1)}, bf16[448,32,512]{2,1,0:T(8,128)(2,1)}) fusion(bf16[448,32,512]{2,1,0:T(8,128)(2,1)} %gather_fusion.1, pred[448]{0:T(512)(128)(4,1)S(1)} %compare_and_fusion, bf16[448,32,512]{2,1,0:T(8,128)(2,1)} %gather_fusion), kind=kLoop, calls=%fused_computation.19 | loop fusion | flops 14680064 | bytes 58720704 | tf_op jit(solution)/shard_map/jit(_take)/select_n | solution.py:20
  747.0 321.5 %all_to_all.58 = bf16[8,1792,512]{2,1,0:T(8,128)(2,1)} all-to-all(bf16[8,1792,512]{2,1,0:T(8,128)(2,1)S(1)} %bitcast.51), channel_id=1, replica_groups=mesh['expert'=4,'unit'=8] {'unit'}, dimensions={0} | all-to-all | bytes 29360128 | tf_op jit(solution)/shard_map/all_to_all | solution.py:28
  1074.7 18.6 %copy.21 = bf16[1,1792,4096]{1,2,0:T(8,128)(2,1)} copy(bf16[1,1792,4096]{2,1,0:T(8,128)(2,1)} %param.8) | data formatting | bytes 29360128 | tf_op args[0]
  1093.4 18.8 %copy.25 = bf16[1,1792,4096]{1,2,0:T(8,128)(2,1)} copy(bf16[1,1792,4096]{2,1,0:T(8,128)(2,1)} %param.9) | data formatting | bytes 29360128 | tf_op args[1]
  1112.1 286.1 %all-gather.3.cloned.1.call-done = bf16[32,4,4096]{2,1,0:T(4,128)(2,1)} async-done(((bf16[1,4,4096]{2,1,0:T(4,128)(2,1)}), bf16[32,4,4096]{2,1,0:T(4,128)(2,1)}) %all-gather.3.cloned.1.call-update) | async-done | bytes 1048592 | tf_op jit(solution)/shard_map/all_gather | solution.py:33
  1399.5 16.8 %convert_bitcast_fusion.2 = f32[1792,8,512]{2,0,1:T(8,128)} fusion(bf16[8,1792,512]{2,1,0:T(8,128)(2,1)} %all_to_all.58), kind=kLoop, calls=%fused_computation.17 | loop fusion | flops 7340032 | bytes 44040192 | tf_op jit(solution)/shard_map/convert_element_type | solution.py:10
  1416.3 27.6 %copy.28 = f32[1792,8,512]{0,2,1:T(8,128)} copy(f32[1792,8,512]{2,0,1:T(8,128)} %convert_bitcast_fusion.2) | data formatting | bytes 58720256 | tf_op jit(solution)/shard_map/convert_element_type | solution.py:10
  1444.0 20.5 %fusion.9 = bf16[1792,4096]{0,1:T(8,128)(2,1)} fusion(bf16[1,1792,4096]{1,2,0:T(8,128)(2,1)} %copy.25, f32[1792,8,512]{0,2,1:T(8,128)} %copy.28), kind=kLoop, calls=%fused_computation.16 | loop fusion | flops 29360128 | bytes 58720256 | tf_op jit(solution)/shard_map/convert_element_type | solution.py:10
  1471.4 14.6 fusion.6
  1486.0 16.8 %convert_bitcast_fusion.3 = f32[1792,8,512]{2,0,1:T(8,128)} fusion(bf16[8,1792,512]{2,1,0:T(8,128)(2,1)} %all-to-all-done.1), kind=kLoop, calls=%fused_computation.18 | loop fusion | flops 7340032 | bytes 44040192 | tf_op jit(solution)/shard_map/convert_element_type | solution.py:10
  1502.8 27.6 %copy.24 = f32[1792,8,512]{0,2,1:T(8,128)} copy(f32[1792,8,512]{2,0,1:T(8,128)} %convert_bitcast_fusion.3) | data formatting | bytes 58720256 | tf_op jit(solution)/shard_map/convert_element_type | solution.py:10
  1530.5 20.5 %fusion.4 = bf16[1792,4096]{0,1:T(8,128)(2,1)} fusion(bf16[1,1792,4096]{1,2,0:T(8,128)(2,1)} %copy.21, f32[1792,8,512]{0,2,1:T(8,128)} %copy.24), kind=kLoop, calls=%fused_computation.11 | loop fusion | flops 29360128 | bytes 58720256 | tf_op jit(solution)/shard_map/convert_element_type | solution.py:10
  1557.9 14.6 fusion.1
  1572.5 20.1 %copy.32 = bf16[1,1792,4096]{2,1,0:T(8,128)(2,1)} copy(bf16[1,1792,4096]{1,2,0:T(8,128)(2,1)} %fusion.6) | data formatting | bytes 29360128
  1592.6 20.1 %copy.31 = bf16[1,1792,4096]{2,1,0:T(8,128)(2,1)} copy(bf16[1,1792,4096]{1,2,0:T(8,128)(2,1)} %fusion.1) | data formatting | bytes 29360128
  1620.0 8.3 fusion.11
  (20 shorter events, 44.6 us)
Async XLA Ops:
  25.8 325.3 %all-to-all-start = ((bf16[1792,8,512]{0,2,1:T(8,128)(2,1)}), bf16[1792,8,512]{0,2,1:T(8,128)(2,1)}, u32[]{:S(2)}, u32[]{:S(2)}) async-start(bf16[1792,8,512]{0,2,1:T(8,128)(2,1)} %bitcast.48), calls=%async_computation | async-start | bytes 29360128 | tf_op jit(solution)/shard_map/all_to_all | solution.py:23
  351.1 5.7 copy-start.2
  351.1 322.8 %all-to-all-start.2 = ((bf16[1792,8,512]{0,2,1:T(8,128)(2,1)}), bf16[1792,8,512]{0,2,1:T(8,128)(2,1)}, u32[]{:S(2)}, u32[]{:S(2)}) async-start(bf16[1792,8,512]{0,2,1:T(8,128)(2,1)} %bitcast.47), calls=%async_computation.2 | async-start | bytes 29360128 | tf_op jit(solution)/shard_map/all_to_all | solution.py:24
  1068.5 417.6 %all-to-all-start.1 = ((bf16[8,1792,512]{2,1,0:T(8,128)(2,1)}), bf16[8,1792,512]{2,1,0:T(8,128)(2,1)}, u32[]{:S(2)}, u32[]{:S(2)}) async-start(bf16[8,1792,512]{2,1,0:T(8,128)(2,1)} %bitcast.49), calls=%async_computation.1 | async-start | bytes 29360128 | tf_op jit(solution)/shard_map/all_to_all | solution.py:27
  1074.0 324.2 %all-gather.3.cloned.1.call-start = ((), (), s32[]{:S(2)}) async-start(), calls=%async_computation.4 | async-start | bytes 1081344 | tf_op jit(solution)/shard_map/all_gather | solution.py:33
  1444.0 27.5 %copy-start = (f32[1792,8,512]{0,2,1:T(8,128)S(1)}, f32[1792,8,512]{0,2,1:T(8,128)}, u32[]{:S(2)}) copy-start(f32[1792,8,512]{0,2,1:T(8,128)} %copy.28) | copy-start | bytes 88080384
  1530.5 27.5 %copy-start.1 = (f32[1792,8,512]{0,2,1:T(8,128)S(1)}, f32[1792,8,512]{0,2,1:T(8,128)}, u32[]{:S(2)}) copy-start(f32[1792,8,512]{0,2,1:T(8,128)} %copy.24) | copy-start | bytes 88080384
Sparse Core Ops, SparseCore 0:
  1077.8 320.3 all-gather.2
where the time goes:
time: 1640 us
  waiting for transfers between devices  881 us (54%)
  blocking collectives  322 us (20%)
  local copies, waits for them, and re-layouts  263 us (16%)
  other arithmetic  121 us (7%)
  starting transfers between devices  18.7 us (1%)
    all_to_all x1, blocking collectives, local(): lax.all_to_all(relocate(gathered[1]), 'unit', split_axis=0, concat_axis=1...  322 us
    all_to_all x1, waiting for transfers between devices, local(): lax.all_to_all(b_gate[0], 'unit', split_axis=1, concat_axis=0, tiled=True)  299 us
    all_to_all x1, waiting for transfers between devices, local(): lax.all_to_all(b_up[0], 'unit', split_axis=1, concat_axis=0, tiled=True)  295 us
    all_gather x1, waiting for transfers between devices, local(): piece = lax.all_gather(calib, ('expert', 'unit'), axis=0, tiled=True)  286 us
    unnamed x13, local copies, waits for them, and re-layouts  130 us
    convert_element_type x4, other arithmetic, average(): ((first.astype(jnp.float32) + second.astype(jnp.float32)) * 0.5).astype(j...  70.3 us
    convert_element_type x2, local copies, waits for them, and re-layouts, average(): second.astype(jnp.float32)  55.3 us
    gather x2, local copies, waits for them, and re-layouts, relocate(): return jnp.take(grouped, inverse, axis=0).reshape(total, columns.shape[1])  37.1 us
  transfers between devices with their start and end apart: 4, of which 3 were waited for; matrix products, arithmetic and copies ran while one was open for 10% of the time, Pallas kernels for 0%

commit v1 on v0

--- a/solution.py
+++ b/solution.py
@@ -30,7 +30,12 @@
     merged_gate = average(a_gate[0], returned[0])
     merged_up = average(a_up[0], returned[1])
     dims = (((1,), (1,)), ((), ()))
-    piece = lax.all_gather(calib, ("expert", "unit"), axis=0, tiled=True)
+    piece = jnp.concatenate(
+        lax.all_to_all(
+            jnp.stack([calib] * lax.axis_size(("expert", "unit"))), ("expert", "unit"), 0, 0
+        ),
+        axis=0,
+    )
     gate_pre = lax.dot_general(merged_gate, piece, dims, preferred_element_type=jnp.float32)
     up_pre = lax.dot_general(merged_up, piece, dims, preferred_element_type=jnp.float32)
     hidden = (jax.nn.silu(gate_pre) * up_pre).astype(jnp.bfloat16)

time: 1640 us -> 1500 us (0.915)
  waiting for transfers between devices: 881 us -> 782 us
  other arithmetic: 121 us -> 96.6 us
    all_gather x1 -> x0, waiting for transfers between devices: 286 us -> none  [local(): piece = lax.all_gather(calib, ('expert', 'unit'), axis=0, tiled=True)]
    all_to_all x1 -> x2, waiting for transfers between devices: 0.01 us -> 188 us  [the longest x1 188 us: local(): lax.all_to_all(relocate(gathered[1]), 'unit', split_axis=0, concat_axis=1...]
    convert_element_type x4 -> x2, other arithmetic: 70.3 us -> 40.9 us  [average(): ((first.astype(jnp.float32) + second.astype(jnp.float32)) * 0.5).astype(j...]
    unnamed x13 -> x10, local copies, waits for them, and re-layouts: 130 us -> 115 us
  transfers between devices with their start and end apart: 4 -> 4, of which waited for: 3 -> 3; matrix products, arithmetic and copies ran while one was open for 10% -> 17% of each run, Pallas kernels for 0% -> 0%
where the time goes in v1:
time: 1500 us; the launch traced here: 1490 us
  waiting for transfers between devices  782 us (52%)
  blocking collectives  326 us (22%)
  local copies, waits for them, and re-layouts  249 us (17%)
  other arithmetic  96.6 us (6%)
  starting transfers between devices  22.3 us (1%)
  matrix products  15.6 us (1%)
    all_to_all x1, blocking collectives, local(): lax.all_to_all(relocate(gathered[0]), 'unit', split_axis=0, concat_axis=1...  326 us
    all_to_all x1, waiting for transfers between devices, local(): lax.all_to_all(b_gate[0], 'unit', split_axis=1, concat_axis=0, tiled=True)  299 us
    all_to_all x1, waiting for transfers between devices, local(): lax.all_to_all(b_up[0], 'unit', split_axis=1, concat_axis=0, tiled=True)  295 us
    all_to_all x1, waiting for transfers between devices, local(): lax.all_to_all(relocate(gathered[1]), 'unit', split_axis=0, concat_axis=1...  188 us
    unnamed x10, local copies, waits for them, and re-layouts  115 us
    convert_element_type x2, local copies, waits for them, and re-layouts, average(): second.astype(jnp.float32)  55.3 us
    convert_element_type x2, other arithmetic, average(): ((first.astype(jnp.float32) + second.astype(jnp.float32)) * 0.5).astype(j...  40.9 us
    gather x2, local copies, waits for them, and re-layouts, relocate(): return jnp.take(grouped, inverse, axis=0).reshape(total, columns.shape[1])  37.1 us
  transfers between devices with their start and end apart: 4, of which 3 were waited for; matrix products, arithmetic and copies ran while one was open for 17% of the time, Pallas kernels for 0%

profile of v1, /device:TPU:0, one launch (start us, length us, event | category | flops | bytes accessed | tf_op | source)
XLA Modules:
  0.0 1492.8 jit_solution(2674051864412226067)
XLA Ops:
  0.6 18.6 %copy.10 = bf16[1,1792,4096]{1,2,0:T(8,128)(2,1)} copy(bf16[1,1792,4096]{2,1,0:T(8,128)(2,1)} %param.10) | data formatting | bytes 29360128 | tf_op args[2]
  19.3 7.3 all-to-all-start
  26.5 18.6 %copy.14 = bf16[1,1792,4096]{1,2,0:T(8,128)(2,1)} copy(bf16[1,1792,4096]{2,1,0:T(8,128)(2,1)} %param.11) | data formatting | bytes 29360128 | tf_op args[3]
  45.2 299.4 %all-to-all-done = bf16[1792,8,512]{0,2,1:T(8,128)(2,1)} async-done(((bf16[1792,8,512]{0,2,1:T(8,128)(2,1)}), bf16[1792,8,512]{0,2,1:T(8,128)(2,1)}, u32[]{:S(2)}, u32[]{:S(2)}) %all-to-all-start) | async-done | bytes 14680096 | tf_op jit(solution)/shard_map/all_to_all | solution.py:23
  353.2 18.7 %copy.11 = bf16[8,1792,512]{2,1,0:T(8,128)(2,1)} copy(bf16[8,1792,512]{1,2,0:T(8,128)(2,1)} %bitcast.3) | data formatting | bytes 29360128 | tf_op jit(solution)/shard_map/all_to_all | solution.py:23
  371.9 295.4 %all-to-all-done.2 = bf16[1792,8,512]{0,2,1:T(8,128)(2,1)} async-done(((bf16[1792,8,512]{0,2,1:T(8,128)(2,1)}), bf16[1792,8,512]{0,2,1:T(8,128)(2,1)}, u32[]{:S(2)}, u32[]{:S(2)}) %all-to-all-start.2) | async-done | bytes 14680096 | tf_op jit(solution)/shard_map/all_to_all | solution.py:24
  672.4 18.7 %copy.15 = bf16[8,1792,512]{2,1,0:T(8,128)(2,1)} copy(bf16[8,1792,512]{1,2,0:T(8,128)(2,1)} %bitcast.9) | data formatting | bytes 29360128 | tf_op jit(solution)/shard_map/all_to_all | solution.py:24
  691.2 18.6 %gather_fusion = bf16[448,32,512]{2,1,0:T(8,128)(2,1)} fusion(bf16[448,32,512]{2,1,0:T(8,128)(2,1)} %bitcast.46, s32[1024]{0:T(1024)S(1)} %pad_clamp_fusion), kind=kCustom, calls=%fused_computation.clone | custom fusion | bytes 29361920 | tf_op jit(solution)/shard_map/jit(_take)/gather | solution.py:20
  709.7 18.6 %gather_fusion.1 = bf16[448,32,512]{2,1,0:T(8,128)(2,1)} fusion(bf16[448,32,512]{2,1,0:T(8,128)(2,1)} %bitcast.48, s32[1024]{0:T(1024)S(1)} %pad_clamp_fusion), kind=kCustom, calls=%fused_computation.1.clone | custom fusion | bytes 29361920 | tf_op jit(solution)/shard_map/jit(_take)/gather | solution.py:20
  728.3 22.1 %broadcast_select_fusion = (bf16[448,32,512]{2,1,0:T(8,128)(2,1)}, bf16[448,32,512]{2,1,0:T(8,128)(2,1)}) fusion(bf16[448,32,512]{2,1,0:T(8,128)(2,1)} %gather_fusion.1, pred[448]{0:T(512)(128)(4,1)S(1)} %compare_and_fusion, bf16[448,32,512]{2,1,0:T(8,128)(2,1)} %gather_fusion), kind=kLoop, calls=%fused_computation.15 | loop fusion | flops 14680064 | bytes 58720704 | tf_op jit(solution)/shard_map/jit(_take)/select_n | solution.py:20
  750.4 325.8 %all_to_all.63 = bf16[8,1792,512]{2,1,0:T(8,128)(2,1)} all-to-all(bf16[8,1792,512]{2,1,0:T(8,128)(2,1)} %bitcast.47), channel_id=1, replica_groups=mesh['expert'=4,'unit'=8] {'unit'}, dimensions={0} | all-to-all | bytes 29360128 | tf_op jit(solution)/shard_map/all_to_all | solution.py:27
  1082.0 18.6 %copy.9 = bf16[1,1792,4096]{1,2,0:T(8,128)(2,1)} copy(bf16[1,1792,4096]{2,1,0:T(8,128)(2,1)} %param.8) | data formatting | bytes 29360128 | tf_op args[0]
  1100.6 18.8 %copy.13 = bf16[1,1792,4096]{1,2,0:T(8,128)(2,1)} copy(bf16[1,1792,4096]{2,1,0:T(8,128)(2,1)} %param.9) | data formatting | bytes 29360128 | tf_op args[1]
  1119.6 16.8 %convert_bitcast_fusion.1 = f32[1792,8,512]{2,0,1:T(8,128)} fusion(bf16[8,1792,512]{2,1,0:T(8,128)(2,1)} %all_to_all.63), kind=kLoop, calls=%fused_computation.10 | loop fusion | flops 7340032 | bytes 44040192 | tf_op jit(solution)/shard_map/convert_element_type | solution.py:10
  1136.4 27.7 %copy.12 = f32[1792,8,512]{0,2,1:T(8,128)} copy(f32[1792,8,512]{2,0,1:T(8,128)} %convert_bitcast_fusion.1) | data formatting | bytes 58720256 | tf_op jit(solution)/shard_map/convert_element_type | solution.py:10
  1164.1 20.4 %fusion.3 = bf16[1,1792,4096]{1,2,0:T(8,128)(2,1)} fusion(f32[1792,8,512]{0,2,1:T(8,128)} %copy.12, bf16[1,1792,4096]{1,2,0:T(8,128)(2,1)} %copy.9), kind=kLoop, calls=%fused_computation.8 | loop fusion | flops 29360128 | bytes 58720256 | tf_op jit(solution)/shard_map/convert_element_type | solution.py:10
  1184.5 20.1 %copy.17 = bf16[1,1792,4096]{2,1,0:T(8,128)(2,1)} copy(bf16[1,1792,4096]{1,2,0:T(8,128)(2,1)} %fusion.3) | data formatting | bytes 29360128
  1204.6 7.3 fusion.6
  1211.9 187.6 %all-to-all-done.3 = bf16[8,1792,512]{2,1,0:T(8,128)(2,1)} async-done(((bf16[8,1792,512]{2,1,0:T(8,128)(2,1)}), bf16[8,1792,512]{2,1,0:T(8,128)(2,1)}, u32[]{:S(2)}, u32[]{:S(2)}) %all-to-all-start.3) | async-done | bytes 14680096 | tf_op jit(solution)/shard_map/all_to_all | solution.py:28
  1399.5 16.8 %convert_bitcast_fusion = f32[1792,8,512]{2,0,1:T(8,128)} fusion(bf16[8,1792,512]{2,1,0:T(8,128)(2,1)} %all-to-all-done.3), kind=kLoop, calls=%fused_computation.9 | loop fusion | flops 7340032 | bytes 44040192 | tf_op jit(solution)/shard_map/convert_element_type | solution.py:10
  1416.3 27.7 %copy.16 = f32[1792,8,512]{0,2,1:T(8,128)} copy(f32[1792,8,512]{2,0,1:T(8,128)} %convert_bitcast_fusion) | data formatting | bytes 58720256 | tf_op jit(solution)/shard_map/convert_element_type | solution.py:10
  1444.0 20.5 %fusion.1 = bf16[1,1792,4096]{1,2,0:T(8,128)(2,1)} fusion(f32[1792,8,512]{0,2,1:T(8,128)} %copy.16, bf16[1,1792,4096]{1,2,0:T(8,128)(2,1)} %copy.13), kind=kLoop, calls=%fused_computation.5 | loop fusion | flops 29360128 | bytes 58720256 | tf_op jit(solution)/shard_map/convert_element_type | solution.py:10
  1464.4 20.1 %copy.18 = bf16[1,1792,4096]{2,1,0:T(8,128)(2,1)} copy(bf16[1,1792,4096]{1,2,0:T(8,128)(2,1)} %fusion.1) | data formatting | bytes 29360128
  1484.5 8.3 fusion.14
  (16 shorter events, 19.7 us)
Async XLA Ops:
  19.3 325.3 %all-to-all-start = ((bf16[1792,8,512]{0,2,1:T(8,128)(2,1)}), bf16[1792,8,512]{0,2,1:T(8,128)(2,1)}, u32[]{:S(2)}, u32[]{:S(2)}) async-start(bf16[1792,8,512]{0,2,1:T(8,128)(2,1)} %bitcast.44), calls=%async_computation | async-start | bytes 29360128 | tf_op jit(solution)/shard_map/all_to_all | solution.py:23
  344.5 5.7 copy-start.1
  344.5 322.8 %all-to-all-start.2 = ((bf16[1792,8,512]{0,2,1:T(8,128)(2,1)}), bf16[1792,8,512]{0,2,1:T(8,128)(2,1)}, u32[]{:S(2)}, u32[]{:S(2)}) async-start(bf16[1792,8,512]{0,2,1:T(8,128)(2,1)} %bitcast.43), calls=%async_computation.2 | async-start | bytes 29360128 | tf_op jit(solution)/shard_map/all_to_all | solution.py:24
  353.2 314.1 %copy-start = (bf16[4,4096]{1,0:T(4,128)(2,1)S(1)}, bf16[4,4096]{1,0:T(4,128)(2,1)}, u32[]{:S(2)}) copy-start(bf16[4,4096]{1,0:T(4,128)(2,1)} %param.13) | copy-start | bytes 98308
  668.8 81.7 %all-to-all-start.4 = ((bf16[32,4,4096]{2,1,0:T(4,128)(2,1)}), bf16[32,4,4096]{2,1,0:T(4,128)(2,1)S(1)}, u32[]{:S(2)}, u32[]{:S(2)}) async-start(bf16[32,4,4096]{2,1,0:T(4,128)(2,1)} %stack.2), calls=%async_computation.4 | async-start | bytes 2097152 | tf_op jit(solution)/shard_map/all_to_all | solution.py:34
  1076.2 323.3 %all-to-all-start.3 = ((bf16[8,1792,512]{2,1,0:T(8,128)(2,1)}), bf16[8,1792,512]{2,1,0:T(8,128)(2,1)}, u32[]{:S(2)}, u32[]{:S(2)}) async-start(bf16[8,1792,512]{2,1,0:T(8,128)(2,1)} %bitcast.45), calls=%async_computation.3 | async-start | bytes 29360128 | tf_op jit(solution)/shard_map/all_to_all | solution.py:28
